TPU v7x, 32 devices: a whole 2x2x4 slice. The times are simulated.
32 devices in a mesh: groups: 2 (over y), axial: 16 (over z, x, core).
Axes of the slice: x: 2, y: 2, z: 4, core: 2. Of those that a mesh axis runs over, the one named last changes fastest.
Arguments:
- pair_rep: bfloat16 [192, 96, 128], P(('groups', 'axial')), parts along dimension 0, may hold values from -6 to 6
- norm_out: float32 [128], replicated, may hold values from 0.5 to 1.5
- proj_out: bfloat16 [128, 512], replicated, may hold values from -0.5 to 0.5
- gate_out: bfloat16 [128, 128], replicated, may hold values from -0.5 to 0.5
- mid_out: float32 [128], replicated, may hold values from 0.5 to 1.5
- final_out: bfloat16 [128, 128], replicated, may hold values from -0.5 to 0.5
- norm_in: float32 [128], replicated, may hold values from 0.5 to 1.5
- proj_in: bfloat16 [128, 512], replicated, may hold values from -0.5 to 0.5
- gate_in: bfloat16 [128, 128], replicated, may hold values from -0.5 to 0.5
- mid_in: float32 [128], replicated, may hold values from 0.5 to 1.5
- final_in: bfloat16 [128, 128], replicated, may hold values from -0.5 to 0.5
Outputs:
- updated: bfloat16 [192, 96, 128], P(('groups', 'axial')), parts along dimension 0
There are 2 independent parts, one for each index of `groups`. A program takes and returns all parts, laid end to end along the dimension named above; an argument that names none is the same for every part. Nothing has to cross between parts.
All inputs are finite; a program needn't handle non-finite values.
Results may differ from a plain program's by a relative error of at most 0.013.
Values may be sent and summed in bfloat16 or wider, within the bound.
A program may use at most 64 MiB of HBM per device.

v0:
```python
import functools

import jax
import jax.numpy as jnp
from jax import lax
from jax.experimental import pallas as pl
from jax.experimental.pallas import tpu as pltpu
from jax.sharding import PartitionSpec as P

EPS = 1e-05


def normalize(values, gain, axis):
    average = jnp.mean(values, axis=axis, keepdims=True)
    spread = jnp.mean(jnp.square(values - average), axis=axis, keepdims=True)
    return (values - average) * lax.rsqrt(spread + EPS) * gain


def channel_product(left_side, right_side, outgoing):
    formula = "kil,kjl->kij" if outgoing else "kli,klj->kij"
    got_left, got_right = (
        lax.all_to_all(left_side, "axial", split_axis=0, concat_axis=1, tiled=True),
        lax.all_to_all(right_side, "axial", split_axis=0, concat_axis=1, tiled=True),
    )
    return jnp.einsum(formula, got_left, got_right, preferred_element_type=jnp.float32)


def update(pair_rep, norm_gain, weights, gate_weight, mid_gain, final_weight, outgoing):
    normed = normalize(pair_rep.astype(jnp.float32), norm_gain, -1).astype(jnp.bfloat16)
    projected = jnp.einsum("rnc,ck->krn", normed, weights, preferred_element_type=jnp.float32)
    hidden = weights.shape[1] // 4
    left_side = (jax.nn.sigmoid(projected[hidden : 2 * hidden]) * projected[:hidden]).astype(
        jnp.bfloat16
    )
    right_side = (
        jax.nn.sigmoid(projected[3 * hidden :]) * projected[2 * hidden : 3 * hidden]
    ).astype(jnp.bfloat16)
    product = channel_product(left_side, right_side, outgoing)
    tri = lax.all_to_all(
        product.astype(jnp.bfloat16), "axial", split_axis=1, concat_axis=0, tiled=True
    )
    gating = jax.nn.sigmoid(
        jnp.einsum("rnc,ce->rne", normed, gate_weight, preferred_element_type=jnp.float32)
    )
    tri_normed = normalize(tri.astype(jnp.float32), mid_gain[:, None, None], 0).astype(jnp.bfloat16)
    result = jnp.einsum("krn,kc->rnc", tri_normed, final_weight, preferred_element_type=jnp.float32)
    return (pair_rep.astype(jnp.float32) + gating * result).astype(jnp.bfloat16)


MESH = pl.DeviceIdType.MESH
CORES = 2
SIDES = 2
UP, DOWN, ACROSS = range(3)
VMEM_BYTES = 56 * 1024 * 1024


def fits(devices, pair_shape, proj_shape):
    rows, tokens, channels = pair_shape
    hidden = proj_shape[1] // 4
    held = 2 * devices * rows * tokens * hidden * 2
    work = 12 * rows * tokens * max(hidden, channels) * 4
    return (
        devices % (CORES * SIDES) == 0
        and devices * rows == tokens
        and rows <= 8
        and tokens % (16 * CORES) == 0
        and channels == hidden
        and hidden % 128 == 0
        and held + work < VMEM_BYTES // 2
    )


def layer_norm(values, gain):
    average = jnp.mean(values, axis=-1, keepdims=True)
    centred = values - average
    spread = jnp.mean(jnp.square(centred), axis=-1, keepdims=True)
    return centred * lax.rsqrt(spread + EPS) * gain


def dot(left, right):
    return jnp.dot(left, right, preferred_element_type=jnp.float32)


def gather_kernel(
    devices,
    pieces,
    pair_ref,
    norm_out,
    proj_out,
    gate_out,
    mid_out,
    final_out,
    norm_in,
    proj_in,
    gate_in,
    mid_in,
    final_in,
    out_ref,
    held,
    columns_out,
    columns_in,
    columns_f32,
    rows_f32,
    left_out,
    left_in,
    left_f32,
    partial,
    tri,
    part_out,
    part_in,
    gating,
    normed_ref,
    send_sem,
    recv_sem,
    columns_send_sem,
    columns_recv_sem,
    peer_send_sem,
    peer_recv_sem,
):
    rows, tokens, channels = pair_ref.shape
    hidden = held.shape[-1]
    chips = devices // CORES
    length = chips // SIDES
    both = CORES * rows
    pad = both
    share = chips * rows
    piece = rows // pieces
    me = lax.axis_index("axial")
    core = me % CORES
    chip = me // CORES
    side = chip % SIDES
    line = chip // SIDES
    low = jnp.minimum(line, length - 1 - line)

    def near(step):
        if step == 0:
            return line
        first = jnp.where(2 * line < length, 1, -1)
        hop = (step + 1) // 2
        pair = line - first * hop if step % 2 else line + first * hop
        alone = jnp.where(2 * line < length, step, length - 1 - step)
        return jnp.where(step <= 2 * low, pair, alone)

    def index(chip_at):
        return chip_at * CORES + core

    order = [near(step) for step in range(length)]
    mine = [at * SIDES + side for at in order]
    beside = [at * SIDES + 1 - side for at in order]
    peer = chip * CORES + 1 - core
    targets = {
        UP: index(jnp.minimum(line + 1, length - 1) * SIDES + side),
        DOWN: index(jnp.maximum(line - 1, 0) * SIDES + side),
        ACROSS: index(line * SIDES + 1 - side),
    }

    def line_event(event):
        step, part = 1 + event // pieces, event % pieces
        at = order[step]
        if event < 2 * pieces and length > 2:
            inner = low >= 1
            at = jnp.where(inner, order[1 + event % 2], at)
            part = jnp.where(inner, event // 2, part)
        return at, part

    def copy(phase, way, block, part):
        window = pl.ds(part * piece, piece)
        return pltpu.make_async_remote_copy(
            src_ref=held.at[phase, block, window],
            dst_ref=held.at[phase, block, window],
            send_sem=send_sem.at[phase, way, block, part],
            recv_sem=recv_sem.at[phase, block, part],
            device_id={"axial": targets[way]},
            device_id_type=MESH,
        )

    def pass_on(phase, at, part, act):
        block = at * SIDES + side

        @pl.when(jnp.logical_and(at <= line, line < length - 1))
        def _():
            act(copy(phase, UP, block, part))

        @pl.when(jnp.logical_and(at >= line, line > 0))
        def _():
            act(copy(phase, DOWN, block, part))

        act(copy(phase, ACROSS, block, part))

    def start(descriptor):
        descriptor.start()

    def finish_send(descriptor):
        descriptor.wait_send()

    def arrived(phase, block, part):
        copy(phase, ACROSS, block, part).wait_recv()

    def columns_copy(block, target):
        return pltpu.make_async_remote_copy(
            src_ref=columns_out.at[target],
            dst_ref=columns_in.at[block],
            send_sem=columns_send_sem.at[target],
            recv_sem=columns_recv_sem.at[block],
            device_id={"axial": index(target)},
            device_id_type=MESH,
        )

    def peer_copy(source, target, which):
        return pltpu.make_async_remote_copy(
            src_ref=source,
            dst_ref=target,
            send_sem=peer_send_sem.at[which],
            recv_sem=peer_recv_sem.at[which],
            device_id={"axial": peer},
            device_id_type=MESH,
        )

    left_copy = peer_copy(left_out, left_in, 0)
    tri_copy = peer_copy(part_out.at[0, :, :share], part_in.at[0, :, :share], 1)
    sum_copy = peer_copy(part_out.at[1], part_in.at[1], 2)

    def exchange(phase, multiply):
        def from_line(step):
            for event in range((step - 1) * pieces, step * pieces):
                at, part = line_event(event)
                arrived(phase, at * SIDES + side, part)
                pass_on(phase, at, part, start)

        def from_side(step):
            for part in range(pieces):
                arrived(phase, beside[step], part)
            multiply(beside[step])

        multiply(mine[0])
        for step in range(1, length):
            from_line(step)
            if step == 2:
                from_side(0)
            if 2 <= step < length - 1:
                multiply(mine[step - 1])
        for step in range(max(1, length - 2), length):
            multiply(mine[step])
        for step in range(1 if length > 2 else 0, length):
            from_side(step)

    def finish_sends(phase):
        for step in range(length):
            for part in range(pieces):
                pass_on(phase, order[step], part, finish_send)

    def split(values):
        return values.reshape(rows, tokens, values.shape[-1])

    def gated(projected):
        return (jax.nn.sigmoid(projected[:, hidden:]) * projected[:, :hidden]).astype(jnp.bfloat16)

    def outgoing_block(block):
        def one(row, carry):
            right = held[0, block, row].astype(jnp.float32)
            at = pl.ds(block * rows + row, 1)
            for half in range(CORES):
                total = jnp.sum(left_f32[half] * right[None], axis=1, keepdims=True)
                partial[half, :, at, :] = total
            return carry

        lax.fori_loop(0, rows, one, 0)

    def incoming_block(block):
        @pl.when(block != chip)
        def _():
            columns_copy(block, chip * 0 + beside[0]).wait_recv()

        rows_f32[...] = columns_in[block].astype(jnp.float32)

        def one(tile, carry):
            window = pl.ds(pl.multiple_of(tile * 16, 16), 16)
            right = held[1, block, :, window, :].astype(jnp.float32)
            for i in range(both):
                total = partial[i // rows, i % rows, window, :]
                for l in range(rows):
                    total = total + rows_f32[pl.ds(l * pad + i, 1), :] * right[l]
                partial[i // rows, i % rows, window, :] = total
            return carry

        lax.fori_loop(0, tokens // 16, one, 0)

    def flat(values):
        return values.reshape(-1, values.shape[-1])

    def close(pair, part, mid_gain, final):
        product = flat(tri[span(part)]).astype(jnp.bfloat16).astype(jnp.float32)
        normed = layer_norm(product, mid_gain[...]).astype(jnp.bfloat16)
        return (pair + gating[flat_span(part)] * dot(normed, final[...])).astype(jnp.bfloat16)

    def span(part):
        return pl.ds(part * piece, piece)

    def flat_span(part):
        return pl.ds(part * piece * tokens, piece * tokens)

    def open_piece(phase, part, pair, norm, proj):
        normed = layer_norm(pair, norm[...]).astype(jnp.bfloat16)
        normed_ref[flat_span(part)] = normed
        right = gated(dot(normed, proj[:, 2 * hidden :]))
        held[phase, chip, span(part)] = right.reshape(piece, tokens, hidden)

    barrier = pltpu.get_barrier_semaphore()
    for offset in range(1, chips):
        pl.semaphore_signal(
            barrier,
            inc=1,
            device_id={"axial": index(lax.rem(chip + offset, chips))},
            device_id_type=MESH,
        )
    pl.semaphore_signal(barrier, inc=1, device_id={"axial": peer}, device_id_type=MESH)

    for part in range(pieces):
        pair = flat(pair_ref[span(part)]).astype(jnp.float32)
        open_piece(0, part, pair, norm_out, proj_out)
        if part == 0:
            pl.semaphore_wait(barrier, chips)
        pass_on(0, line, part, start)
    left_out[...] = split(gated(dot(normed_ref[...], proj_out[:, : 2 * hidden])))
    left_copy.start()
    left_f32[0] = left_out[...].astype(jnp.float32)
    gating[...] = jax.nn.sigmoid(dot(normed_ref[...], gate_out[...]))
    left_copy.wait_recv()
    left_f32[1] = left_in[...].astype(jnp.float32)
    exchange(0, outgoing_block)
    part_out[0, :, :share] = partial[1, :, :share].astype(jnp.bfloat16)
    tri_copy.start()
    tri_copy.wait_recv()
    partial[1, :, :share] = part_in[0, :, :share].astype(jnp.float32)
    for half in range(CORES):
        for block in range(chips):
            at = (block * CORES + half) * rows
            got = pl.ds(block * rows, rows)
            tri[:, at : at + rows, :] = jnp.where(
                core == half, partial[0, :, got, :], partial[1, :, got, :]
            )
    for part in range(pieces):
        pair = flat(pair_ref[span(part)]).astype(jnp.float32)
        first = close(pair, part, mid_out, final_out)
        out_ref[span(part)] = first.reshape(piece, tokens, channels)
        open_piece(1, part, first.astype(jnp.float32), norm_in, proj_in)
        pass_on(1, line, part, start)
    left_f32[0] = split(gated(dot(normed_ref[...], proj_in[:, : 2 * hidden]))).astype(jnp.float32)
    columns_f32[...] = jnp.zeros_like(columns_f32)
    for target in range(chips):
        for l in range(rows):
            columns_f32[target, l * pad : l * pad + both, :] = left_f32[
                0, l, target * both : (target + 1) * both, :
            ]
    columns_out[...] = columns_f32[...].astype(jnp.bfloat16)
    for offset in range(1, chips):
        columns_copy(chip, lax.rem(chip + offset, chips)).start()
    columns_in[chip] = columns_out[chip]
    gating[...] = jax.nn.sigmoid(dot(normed_ref[...], gate_in[...]))
    partial[...] = jnp.zeros_like(partial)
    exchange(1, incoming_block)
    part_out[1] = partial[1 - core].astype(jnp.bfloat16)
    sum_copy.start()
    sum_copy.wait_recv()
    tri[...] = partial[core] + part_in[1].astype(jnp.float32)
    for part in range(pieces):
        again = flat(out_ref[span(part)]).astype(jnp.float32)
        out_ref[span(part)] = close(again, part, mid_in, final_in).reshape(piece, tokens, channels)

    for offset in range(1, chips):
        columns_copy(chip, lax.rem(chip + offset, chips)).wait_send()
    left_copy.wait_send()
    tri_copy.wait_send()
    sum_copy.wait_send()
    finish_sends(0)
    finish_sends(1)


def gather_rows(devices, pair_rep, *weights):
    rows, tokens, channels = pair_rep.shape
    hidden = weights[1].shape[1] // 4
    gains = [w.reshape(1, -1) if w.ndim == 1 else w for w in weights]
    chips = devices // CORES
    packed = -(-CORES * rows * rows // 16) * 16
    pieces = next(count for count in (3, 2, 1) if rows % count == 0)
    block = (rows, tokens, hidden)
    return pl.pallas_call(
        functools.partial(gather_kernel, devices, pieces),
        out_shape=jax.ShapeDtypeStruct(pair_rep.shape, pair_rep.dtype),
        in_specs=[pl.BlockSpec(memory_space=pltpu.VMEM)] * 11,
        out_specs=pl.BlockSpec(memory_space=pltpu.VMEM),
        scratch_shapes=[
            pltpu.VMEM((2, chips) + block, jnp.bfloat16),
            pltpu.VMEM((chips, packed, hidden), jnp.bfloat16),
            pltpu.VMEM((chips, packed, hidden), jnp.bfloat16),
            pltpu.VMEM((chips, packed, hidden), jnp.float32),
            pltpu.VMEM((packed, hidden), jnp.float32),
            pltpu.VMEM(block, jnp.bfloat16),
            pltpu.VMEM(block, jnp.bfloat16),
            pltpu.VMEM((CORES,) + block, jnp.float32),
            pltpu.VMEM((CORES,) + block, jnp.float32),
            pltpu.VMEM(block, jnp.float32),
            pltpu.VMEM((2,) + block, jnp.bfloat16),
            pltpu.VMEM((2,) + block, jnp.bfloat16),
            pltpu.VMEM((rows * tokens, channels), jnp.float32),
            pltpu.VMEM((rows * tokens, channels), jnp.bfloat16),
            pltpu.SemaphoreType.DMA((2, 3, chips, pieces)),
            pltpu.SemaphoreType.DMA((2, chips, pieces)),
            pltpu.SemaphoreType.DMA((chips,)),
            pltpu.SemaphoreType.DMA((chips,)),
            pltpu.SemaphoreType.DMA((3,)),
            pltpu.SemaphoreType.DMA((3,)),
        ],
        compiler_params=pltpu.CompilerParams(
            collective_id=0, has_side_effects=True, vmem_limit_bytes=VMEM_BYTES
        ),
        name="gather_rows",
    )(pair_rep, *gains)


def exchange_channels(
    pair_rep,
    norm_out,
    proj_out,
    gate_out,
    mid_out,
    final_out,
    norm_in,
    proj_in,
    gate_in,
    mid_in,
    final_in,
):
    first = update(pair_rep, norm_out, proj_out, gate_out, mid_out, final_out, True)
    return update(first, norm_in, proj_in, gate_in, mid_in, final_in, False)


def solution(mesh):
    devices = mesh.shape["axial"]

    def on_device(*arrays):
        if fits(devices, arrays[0].shape, arrays[2].shape):
            return gather_rows(devices, *arrays)
        return exchange_channels(*arrays)

    placed = (P(("groups", "axial"), None, None), P(), P(), P(), P(), P(), P(), P(), P(), P(), P())
    return jax.shard_map(
        on_device,
        mesh=mesh,
        in_specs=placed,
        out_specs=P(("groups", "axial"), None, None),
        check_vma=False,
    )
```

profile of v0, /device:TPU:0, one launch (start us, length us, event | category | flops | bytes accessed | tf_op | source)
XLA Modules:
  0.0 45.7 jit_solution(4849115211179453116)
XLA Ops:
  0.0 44.1 %gather_rows.1 = bf16[6,96,128]{2,1,0:T(8,128)(2,1)} custom-call(bf16[6,96,128]{2,1,0:T(8,128)(2,1)} %pair_ref.1, f32[1,128]{1,0:T(1,128)} %bitcast.4, bf16[128,512]{1,0:T(8,128)(2,1)} %proj_out.1, bf16[128,128]{1,0:T(8,128)(2,1)} %gate_out.1, f32[1,128]{1,0:T(1,128)} %bitcast.5, bf16[128,128]{1,0:T(8,128)(2,1)} %final_out.1, f32[1,128]{1,0:T(1,128)} %bitcast.6, ...), custom_call_target="tpu_custom_call" | custom-call | tf_op jit(solution)/shard_map/gather_rows/pallas_call | solution.py:387
  44.1 1.6 %copy.13 = bf16[6,96,128]{2,1,0:T(8,128)(2,1)} copy(bf16[6,96,128]{2,1,0:T(8,128)(2,1)} %gather_rows.1) | data formatting | bytes 294912
where the time goes:
time: 46.1 us; the launch traced here: 45.7 us
  Pallas kernels  44.1 us (96%)
  local copies, waits for them, and re-layouts  1.58 us (3%)
    pallas_call x1, Pallas kernels, gather_rows(): pl.pallas_call(functools.partial(gather_kernel, devices, pieces), out_sha...  44.1 us
    unnamed x1, local copies, waits for them, and re-layouts  1.58 us

commit v1 on v0

v1 whole, which is shorter than its diff:
```python
import functools

import jax
import jax.numpy as jnp
from jax import lax
from jax.experimental import pallas as pl
from jax.experimental.pallas import tpu as pltpu
from jax.sharding import PartitionSpec as P

EPS = 1e-05


def normalize(values, gain, axis):
    average = jnp.mean(values, axis=axis, keepdims=True)
    spread = jnp.mean(jnp.square(values - average), axis=axis, keepdims=True)
    return (values - average) * lax.rsqrt(spread + EPS) * gain


def channel_product(left_side, right_side, outgoing):
    formula = "kil,kjl->kij" if outgoing else "kli,klj->kij"
    got_left, got_right = (
        lax.all_to_all(left_side, "axial", split_axis=0, concat_axis=1, tiled=True),
        lax.all_to_all(right_side, "axial", split_axis=0, concat_axis=1, tiled=True),
    )
    return jnp.einsum(formula, got_left, got_right, preferred_element_type=jnp.float32)


def update(pair_rep, norm_gain, weights, gate_weight, mid_gain, final_weight, outgoing):
    normed = normalize(pair_rep.astype(jnp.float32), norm_gain, -1).astype(jnp.bfloat16)
    projected = jnp.einsum("rnc,ck->krn", normed, weights, preferred_element_type=jnp.float32)
    hidden = weights.shape[1] // 4
    left_side = (jax.nn.sigmoid(projected[hidden : 2 * hidden]) * projected[:hidden]).astype(
        jnp.bfloat16
    )
    right_side = (
        jax.nn.sigmoid(projected[3 * hidden :]) * projected[2 * hidden : 3 * hidden]
    ).astype(jnp.bfloat16)
    product = channel_product(left_side, right_side, outgoing)
    tri = lax.all_to_all(
        product.astype(jnp.bfloat16), "axial", split_axis=1, concat_axis=0, tiled=True
    )
    gating = jax.nn.sigmoid(
        jnp.einsum("rnc,ce->rne", normed, gate_weight, preferred_element_type=jnp.float32)
    )
    tri_normed = normalize(tri.astype(jnp.float32), mid_gain[:, None, None], 0).astype(jnp.bfloat16)
    result = jnp.einsum("krn,kc->rnc", tri_normed, final_weight, preferred_element_type=jnp.float32)
    return (pair_rep.astype(jnp.float32) + gating * result).astype(jnp.bfloat16)


MESH = pl.DeviceIdType.MESH
CORES = 2
SIDES = 2
QUAD = CORES * SIDES
UP, DOWN = range(2)
OWN, PEER, ACROSS, CORNER = range(4)
NEAR, FAR, ALL = (OWN, PEER), (ACROSS, CORNER), (OWN, PEER, ACROSS, CORNER)
SUB = 8
LINE = 4
PIECES = 3
VMEM_BYTES = 56 * 1024 * 1024


def fits(devices, pair_shape, proj_shape):
    rows, tokens, channels = pair_shape
    hidden = proj_shape[1] // 4
    block = rows * tokens * hidden * 4
    return (
        devices == QUAD * LINE
        and devices * rows == tokens
        and rows <= SUB
        and rows % PIECES == 0
        and tokens % 16 == 0
        and channels == hidden
        and hidden % 128 == 0
        and (4 * (devices // QUAD) + 24) * block < VMEM_BYTES // 2
    )


def layer_norm(values, gain):
    average = jnp.mean(values, axis=-1, keepdims=True)
    centred = values - average
    spread = jnp.mean(jnp.square(centred), axis=-1, keepdims=True)
    return centred * lax.rsqrt(spread + EPS) * gain


def dot(left, right):
    return jnp.dot(left, right, preferred_element_type=jnp.float32)


def line_kernel(
    devices,
    pieces,
    pair_ref,
    norm_out,
    proj_out,
    gate_out,
    mid_out,
    final_out,
    norm_in,
    proj_in,
    gate_in,
    mid_in,
    final_in,
    out_ref,
    held,
    fixed,
    fixed_f32,
    moving,
    normed_ref,
    raw_ref,
    resid,
    gating,
    tri,
    closed,
    landed,
    turned,
    line_send,
    line_recv,
    fixed_send,
    fixed_recv,
    closed_send,
    closed_recv,
):
    rows, tokens, channels = pair_ref.shape
    hidden = fixed.shape[-1]
    length = devices // QUAD
    piece = rows // pieces
    me = lax.axis_index("axial")
    core = me % CORES
    side = (me // CORES) % SIDES
    line = me // QUAD
    seats = (
        side * CORES + core,
        side * CORES + 1 - core,
        (1 - side) * CORES + core,
        (1 - side) * CORES + 1 - core,
    )
    seat = seats[OWN]

    def mate(which):
        return line * QUAD + seats[which]

    targets = {
        UP: jnp.minimum(line + 1, length - 1) * QUAD + seat,
        DOWN: jnp.maximum(line - 1, 0) * QUAD + seat,
    }

    inner = jnp.logical_and(line > 0, line < length - 1)
    onward = jnp.where(2 * line < length, 1, -1)
    first_block = line + onward
    second_block = jnp.where(inner, line - onward, line)
    third_block = line + 2 * onward
    fourth_block = jnp.where(inner, line, line + 3 * onward)

    def remote(source, target, sent, got, device):
        return pltpu.make_async_remote_copy(
            src_ref=source,
            dst_ref=target,
            send_sem=sent,
            recv_sem=got,
            device_id={"axial": device},
            device_id_type=MESH,
        )

    def window(part):
        return pl.ds(part * piece, piece)

    def line_copy(phase, way, block, part, source=None):
        there = held.at[phase, block, window(part)]
        return remote(
            there if source is None else source.at[window(part)],
            there,
            line_send.at[phase, way, block, part],
            line_recv.at[phase, block, part],
            targets[way],
        )

    def pass_on(phase, block, part, act, source=None):
        @pl.when(jnp.logical_and(block <= line, line < length - 1))
        def _():
            act(line_copy(phase, UP, block, part, source))

        @pl.when(jnp.logical_and(block >= line, line > 0))
        def _():
            act(line_copy(phase, DOWN, block, part, source))

    def start(descriptor):
        descriptor.start()

    def finish_send(descriptor):
        descriptor.wait_send()

    def fixed_copy(phase, which, to):
        there = fixed.at[phase, seats[which]]
        return remote(
            there,
            there,
            fixed_send.at[phase, which, to],
            fixed_recv.at[phase, seats[which]],
            mate(to),
        )

    def closed_copy(phase, block, which, span):
        return remote(
            closed.at[phase, block, which, span],
            landed.at[phase, block, seat, span],
            closed_send.at[phase, block, which],
            closed_recv.at[phase, block, seat],
            mate(which),
        )

    def closed_wait(phase, block, which):
        remote(
            closed.at[phase, block, which],
            landed.at[phase, block, seats[which]],
            closed_send.at[phase, block, which],
            closed_recv.at[phase, block, seats[which]],
            mate(which),
        ).wait_recv()

    def flat(values):
        return values.reshape(-1, values.shape[-1])

    def gated(projected):
        return (jax.nn.sigmoid(projected[:, hidden:]) * projected[:, :hidden]).astype(jnp.bfloat16)

    def own_side(phase, block, norm, weights):
        normed = layer_norm(flat(block).astype(jnp.float32), norm[...]).astype(jnp.bfloat16)
        made = gated(dot(normed, weights)).reshape(rows, tokens, hidden)
        fixed[phase, seat] = made
        fixed_f32[OWN] = made.astype(jnp.float32)

    def take_fixed(phase, which):
        fixed_copy(phase, which, PEER).wait_recv()
        fixed_f32[which] = fixed[phase, seats[which]].astype(jnp.float32)

    def prepare(phase, block, first, count, norm, weights, gate):
        span = pl.ds(first, count)
        raw = held[phase, block, span].astype(jnp.float32)
        normed = layer_norm(flat(raw), norm[...])
        raw_ref[:count, :tokens] = raw
        normed_ref[:count, :tokens] = normed.reshape(count, tokens, channels)
        made = gated(dot(normed.astype(jnp.bfloat16), weights))
        moving[block, span] = made.astype(jnp.float32).reshape(count, tokens, hidden)
        picked = []
        for row in range(count):
            for which in range(QUAD):
                at = pl.ds(line * (QUAD * rows) + seats[which] * rows, SUB)
                picked.append(normed_ref[row, at, :])
                resid[block, first + row, which] = raw_ref[row, at, :]
        picked = jnp.concatenate(picked, axis=0).astype(jnp.bfloat16)
        opened = jax.nn.sigmoid(dot(picked, gate[...]))
        gating[block, span] = opened.reshape(count, QUAD, SUB, channels)

    def multiply(phase, block, first, count, group, mid, final):
        def one(row, carry):
            right = moving[block, first + row]
            for which in group:
                total = jnp.sum(fixed_f32[which] * right[None], axis=1)
                tri[row, which, :rows, :] = total
            return carry

        lax.fori_loop(0, count, one, 0)
        lanes = slice(group[0], group[0] + len(group))
        product = flat(tri[:count, lanes]).astype(jnp.bfloat16).astype(jnp.float32)
        normed = layer_norm(product, mid[...]).astype(jnp.bfloat16)
        result = dot(normed, final[...]).reshape(count, len(group), SUB, channels)
        span = pl.ds(first, count)
        result = resid[block, span, lanes] + gating[block, span, lanes] * result
        result = result.astype(jnp.bfloat16)
        for place, which in enumerate(group):
            if which == OWN:
                landed[phase, block, seat, span] = result[:, place]
            else:
                closed[phase, block, which, span] = result[:, place]
        for which in group:
            if which != OWN:
                closed_copy(phase, block, which, span).start()

    def exchange(phase, norm, weights, gate, mid, final):
        def ready(block, first=0, count=rows):
            prepare(phase, block, first, count, norm, weights, gate)

        def join(block, group, first=0, count=rows):
            multiply(phase, block, first, count, group, mid, final)

        def arrive(block, part):
            line_copy(phase, UP, block, part).wait_recv()
            pass_on(phase, block, part, start)

        def slot(at):
            step, part = at // pieces, at % pieces
            if step == 0:
                arrive(first_block, part)

                @pl.when(inner)
                def _():
                    arrive(second_block, part)
            elif step == 1:
                arrive(third_block, part)
            else:

                @pl.when(jnp.logical_not(inner))
                def _():
                    arrive(fourth_block, part)

        ready(line)
        take_fixed(phase, PEER)
        join(line, NEAR)
        for at in range(pieces):
            slot(at)
        take_fixed(phase, ACROSS)
        fixed_copy(phase, ACROSS, PEER).start()
        ready(first_block)
        take_fixed(phase, CORNER)
        join(line, FAR)
        slot(pieces)
        join(first_block, ALL)
        slot(pieces + 1)

        @pl.when(inner)
        def _():
            ready(second_block)
            join(second_block, ALL)

        slot(pieces + 2)
        ready(third_block)
        join(third_block, ALL)
        for at in range(2 * pieces, 3 * pieces):
            slot(at)
            if at % pieces:

                @pl.when(jnp.logical_not(inner))
                def _():
                    begin = 0 if at % pieces == 1 else 2 * piece
                    count = 2 * piece if begin == 0 else piece
                    ready(fourth_block, begin, count)
                    join(fourth_block, ALL, begin, count)
        for block in range(length):
            for which in (PEER, ACROSS, CORNER):
                closed_wait(phase, block, which)

    def turn(phase, target, lead):
        turned[...] = landed[phase].reshape(tokens * SUB, channels).astype(jnp.float32)
        for row in range(rows):
            target[lead + (row,)] = turned[pl.ds(row, tokens, stride=SUB), :].astype(jnp.bfloat16)

    def finish(phase, source):
        for block in range(length):
            for part in range(pieces):
                pass_on(phase, block, part, finish_send)
            for which in (PEER, ACROSS, CORNER):
                closed_copy(phase, block, which, pl.ds(0, rows)).wait_send()
        fixed_copy(phase, OWN, PEER).wait_send()
        fixed_copy(phase, OWN, ACROSS).wait_send()
        fixed_copy(phase, ACROSS, PEER).wait_send()

    barrier = pltpu.get_barrier_semaphore()

    def greet(device):
        pl.semaphore_signal(barrier, inc=1, device_id={"axial": device}, device_id_type=MESH)

    for which in (PEER, ACROSS, CORNER):
        greet(mate(which))

    @pl.when(line < length - 1)
    def _():
        greet(targets[UP])

    @pl.when(line > 0)
    def _():
        greet(targets[DOWN])

    held[0, line] = pair_ref[...]
    tri[...] = jnp.zeros_like(tri)
    normed_ref[...] = jnp.zeros_like(normed_ref)
    raw_ref[...] = jnp.zeros_like(raw_ref)
    half = 2 * hidden
    own_side(0, pair_ref[...], norm_out, proj_out[:, half:])
    ends = (line > 0).astype(jnp.int32) + (line < length - 1).astype(jnp.int32)
    pl.semaphore_wait(barrier, QUAD - 1 + ends)
    for part in range(pieces):
        pass_on(0, line, part, start, pair_ref)
    fixed_copy(0, OWN, ACROSS).start()
    fixed_copy(0, OWN, PEER).start()
    exchange(0, norm_out, proj_out[:, :half], gate_out, mid_out, final_out)
    turn(0, held, (1, line))
    for part in range(pieces):
        pass_on(1, line, part, start)
    own_side(1, held[1, line], norm_in, proj_in[:, :half])
    fixed_copy(1, OWN, ACROSS).start()
    fixed_copy(1, OWN, PEER).start()
    exchange(1, norm_in, proj_in[:, half:], gate_in, mid_in, final_in)
    turn(1, out_ref, ())
    finish(0, pair_ref)
    finish(1, held)


def gather_rows(devices, pair_rep, *weights):
    rows, tokens, channels = pair_rep.shape
    hidden = weights[1].shape[1] // 4
    gains = [w.reshape(1, -1) if w.ndim == 1 else w for w in weights]
    length = devices // QUAD
    pieces = PIECES
    block = (rows, tokens, hidden)
    low, full = jnp.bfloat16, jnp.float32
    spot = (QUAD, rows, SUB, channels)
    return pl.pallas_call(
        functools.partial(line_kernel, devices, pieces),
        out_shape=jax.ShapeDtypeStruct(pair_rep.shape, pair_rep.dtype),
        in_specs=[pl.BlockSpec(memory_space=pltpu.VMEM)] * 11,
        out_specs=pl.BlockSpec(memory_space=pltpu.VMEM),
        scratch_shapes=[
            pltpu.VMEM((2, length) + block, low),
            pltpu.VMEM((2, QUAD) + block, low),
            pltpu.VMEM((QUAD,) + block, full),
            pltpu.VMEM((length,) + block, full),
            pltpu.VMEM((rows, tokens + SUB, channels), full),
            pltpu.VMEM((rows, tokens + SUB, channels), full),
            pltpu.VMEM((length, rows, QUAD, SUB, channels), full),
            pltpu.VMEM((length, rows, QUAD, SUB, channels), full),
            pltpu.VMEM((rows, QUAD, SUB, channels), full),
            pltpu.VMEM((2, length) + spot, low),
            pltpu.VMEM((2, length) + spot, low),
            pltpu.VMEM((tokens * SUB, channels), full),
            pltpu.SemaphoreType.DMA((2, 2, length, pieces)),
            pltpu.SemaphoreType.DMA((2, length, pieces)),
            pltpu.SemaphoreType.DMA((2, QUAD, QUAD)),
            pltpu.SemaphoreType.DMA((2, QUAD)),
            pltpu.SemaphoreType.DMA((2, length, QUAD)),
            pltpu.SemaphoreType.DMA((2, length, QUAD)),
        ],
        compiler_params=pltpu.CompilerParams(
            collective_id=0, has_side_effects=True, vmem_limit_bytes=VMEM_BYTES
        ),
        name="gather_rows",
    )(pair_rep, *gains)


def exchange_channels(
    pair_rep,
    norm_out,
    proj_out,
    gate_out,
    mid_out,
    final_out,
    norm_in,
    proj_in,
    gate_in,
    mid_in,
    final_in,
):
    first = update(pair_rep, norm_out, proj_out, gate_out, mid_out, final_out, True)
    return update(first, norm_in, proj_in, gate_in, mid_in, final_in, False)


def solution(mesh):
    devices = mesh.shape["axial"]

    def on_device(*arrays):
        if fits(devices, arrays[0].shape, arrays[2].shape):
            return gather_rows(devices, *arrays)
        return exchange_channels(*arrays)

    placed = (P(("groups", "axial"), None, None), P(), P(), P(), P(), P(), P(), P(), P(), P(), P())
    return jax.shard_map(
        on_device,
        mesh=mesh,
        in_specs=placed,
        out_specs=P(("groups", "axial"), None, None),
        check_vma=False,
    )
```

time: 46.1 us -> 41.8 us (0.907)
  Pallas kernels: 44.1 us -> 40 us
    pallas_call x1, Pallas kernels: 44.1 us -> 40 us  [gather_rows(): pl.pallas_call(functools.partial(line_kernel, devices, pieces), out_shape...]
where the time goes in v1:
time: 41.8 us; the launch traced here: 41.6 us
  Pallas kernels  40 us (96%)
  local copies, waits for them, and re-layouts  1.58 us (4%)
    pallas_call x1, Pallas kernels, gather_rows(): pl.pallas_call(functools.partial(line_kernel, devices, pieces), out_shape...  40 us
    unnamed x1, local copies, waits for them, and re-layouts  1.58 us

profile of v1, /device:TPU:0, one launch (start us, length us, event | category | flops | bytes accessed | tf_op | source)
XLA Modules:
  0.0 41.6 jit_solution(17730434065785457852)
XLA Ops:
  0.0 40.0 %gather_rows.1 = bf16[6,96,128]{2,1,0:T(8,128)(2,1)} custom-call(bf16[6,96,128]{2,1,0:T(8,128)(2,1)} %pair_ref.1, f32[1,128]{1,0:T(1,128)} %bitcast.4, bf16[128,512]{1,0:T(8,128)(2,1)} %proj_out.1, bf16[128,128]{1,0:T(8,128)(2,1)} %gate_out.1, f32[1,128]{1,0:T(1,128)} %bitcast.5, bf16[128,128]{1,0:T(8,128)(2,1)} %final_out.1, f32[1,128]{1,0:T(1,128)} %bitcast.6, ...), custom_call_target="tpu_custom_call" | custom-call | tf_op jit(solution)/shard_map/gather_rows/pallas_call | solution.py:408
  40.1 1.6 %copy.13 = bf16[6,96,128]{2,1,0:T(8,128)(2,1)} copy(bf16[6,96,128]{2,1,0:T(8,128)(2,1)} %gather_rows.1) | data formatting | bytes 294912

commit v2 on v1

v2 whole, which is shorter than its diff:
```python
import functools

import jax
import jax.numpy as jnp
from jax import lax
from jax.experimental import pallas as pl
from jax.experimental.pallas import tpu as pltpu
from jax.sharding import PartitionSpec as P

EPS = 1e-05


def normalize(values, gain, axis):
    average = jnp.mean(values, axis=axis, keepdims=True)
    spread = jnp.mean(jnp.square(values - average), axis=axis, keepdims=True)
    return (values - average) * lax.rsqrt(spread + EPS) * gain


def channel_product(left_side, right_side, outgoing):
    formula = "kil,kjl->kij" if outgoing else "kli,klj->kij"
    got_left, got_right = (
        lax.all_to_all(left_side, "axial", split_axis=0, concat_axis=1, tiled=True),
        lax.all_to_all(right_side, "axial", split_axis=0, concat_axis=1, tiled=True),
    )
    return jnp.einsum(formula, got_left, got_right, preferred_element_type=jnp.float32)


def update(pair_rep, norm_gain, weights, gate_weight, mid_gain, final_weight, outgoing):
    normed = normalize(pair_rep.astype(jnp.float32), norm_gain, -1).astype(jnp.bfloat16)
    projected = jnp.einsum("rnc,ck->krn", normed, weights, preferred_element_type=jnp.float32)
    hidden = weights.shape[1] // 4
    left_side = (jax.nn.sigmoid(projected[hidden : 2 * hidden]) * projected[:hidden]).astype(
        jnp.bfloat16
    )
    right_side = (
        jax.nn.sigmoid(projected[3 * hidden :]) * projected[2 * hidden : 3 * hidden]
    ).astype(jnp.bfloat16)
    product = channel_product(left_side, right_side, outgoing)
    tri = lax.all_to_all(
        product.astype(jnp.bfloat16), "axial", split_axis=1, concat_axis=0, tiled=True
    )
    gating = jax.nn.sigmoid(
        jnp.einsum("rnc,ce->rne", normed, gate_weight, preferred_element_type=jnp.float32)
    )
    tri_normed = normalize(tri.astype(jnp.float32), mid_gain[:, None, None], 0).astype(jnp.bfloat16)
    result = jnp.einsum("krn,kc->rnc", tri_normed, final_weight, preferred_element_type=jnp.float32)
    return (pair_rep.astype(jnp.float32) + gating * result).astype(jnp.bfloat16)


MESH = pl.DeviceIdType.MESH
CORES = 2
SIDES = 2
QUAD = CORES * 2
SAME, SIDE, OVER, BOTH = range(4)
OWN, PEER, ACROSS, CORNER = range(4)
NEAR, FAR, ALL = (OWN, PEER), (ACROSS, CORNER), (OWN, PEER, ACROSS, CORNER)
SUB = 8
HALVES = 2
INPUTS = 11
PIECES = 6
VMEM_BYTES = 56 * 1024 * 1024


def fits(devices, pair_shape, proj_shape):
    rows, tokens, channels = pair_shape
    hidden = proj_shape[1] // 4
    block = rows * tokens * hidden * 4
    return (
        devices == QUAD * SIDES * HALVES
        and devices * rows == tokens
        and rows <= SUB
        and rows % PIECES == 0
        and tokens % 16 == 0
        and channels == hidden
        and hidden % 128 == 0
        and (6 * (devices // QUAD) + 24) * block < VMEM_BYTES // 2
    )


def layer_norm(values, gain):
    average = jnp.mean(values, axis=-1, keepdims=True)
    centred = values - average
    spread = jnp.mean(jnp.square(centred), axis=-1, keepdims=True)
    return centred * lax.rsqrt(spread + EPS) * gain


def dot(left, right):
    return jnp.dot(left, right, preferred_element_type=jnp.float32)


def line_kernel(
    devices,
    pieces,
    *refs,
):
    inputs, out_ref, scratch = refs[:INPUTS], refs[INPUTS], refs[INPUTS + 1 :]
    copies, scratch = scratch[:INPUTS], scratch[INPUTS:]
    (
        pair_ref,
        norm_out,
        proj_out,
        gate_out,
        mid_out,
        final_out,
        norm_in,
        proj_in,
        gate_in,
        mid_in,
        final_in,
    ) = copies
    (
    loaded,
    held,
    fixed,
    fixed_f32,
    moving,
    normed_ref,
    raw_ref,
    resid,
    gating,
    tri,
    closed,
    landed,
    turned,
    line_send,
    line_recv,
    fixed_send,
    fixed_recv,
    closed_send,
    closed_recv,
    ) = scratch
    rows, tokens, channels = pair_ref.shape
    hidden = fixed.shape[-1]
    blocks = devices // QUAD
    piece = rows // pieces
    me = lax.axis_index("axial")
    core = me % CORES
    side = (me // CORES) % SIDES
    level = me // (CORES * SIDES)
    half, floor = level // 2, level % 2
    end = jnp.logical_or(level == 0, level == 2 * HALVES - 1)
    places = ((0, 0), (0, 1), (1, 0), (1, 1))
    seats = ((0, 0), (0, 1), (1, 1), (1, 0))

    def turned_to(value, flip):
        return 1 - value if flip else value

    def device(block, which):
        over, aside = places[block]
        up, swap = seats[which]
        at = 2 * turned_to(half, over) + turned_to(floor, up)
        return (at * SIDES + turned_to(side, aside)) * CORES + turned_to(core, swap != aside)

    def mate(which):
        return device(SAME, which)

    def remote(source, target, sent, got, device):
        return pltpu.make_async_remote_copy(
            src_ref=source,
            dst_ref=target,
            send_sem=sent,
            recv_sem=got,
            device_id={"axial": device},
            device_id_type=MESH,
        )

    def window(part):
        return pl.ds(part * piece, piece)

    def line_copy(phase, target, part, source=None):
        came = held.at[phase, OVER, window(part)]
        goes = came if target == BOTH else source.at[window(part)]
        return remote(
            goes,
            held.at[phase, target, window(part)],
            line_send.at[phase, target, part],
            line_recv.at[phase, target, part],
            device(OVER if target == OVER else SIDE, OWN),
        )

    def fixed_copy(phase, which, to):
        arrives = {(OWN, PEER): PEER, (OWN, ACROSS): ACROSS, (ACROSS, PEER): CORNER}[which, to]
        return remote(
            fixed.at[phase, which],
            fixed.at[phase, arrives],
            fixed_send.at[phase, arrives],
            fixed_recv.at[phase, arrives],
            mate(to),
        )

    def closed_copy(phase, block, which, span):
        here = device(block, OWN)
        return remote(
            closed.at[phase, block, which, span],
            landed.at[phase, here, span],
            closed_send.at[phase, block, which],
            closed_recv.at[phase, here],
            mate(which),
        )

    def closed_wait(phase, block, which):
        there = device(block, which)
        remote(
            closed.at[phase, block, which],
            landed.at[phase, there],
            closed_send.at[phase, block, which],
            closed_recv.at[phase, there],
            mate(which),
        ).wait_recv()

    def flat(values):
        return values.reshape(-1, values.shape[-1])

    def gated(projected):
        return (jax.nn.sigmoid(projected[:, hidden:]) * projected[:, :hidden]).astype(jnp.bfloat16)

    def own_side(phase, block, norm, weights):
        normed = layer_norm(flat(block).astype(jnp.float32), norm[...]).astype(jnp.bfloat16)
        made = gated(dot(normed, weights)).reshape(rows, tokens, hidden)
        fixed[phase, OWN] = made
        fixed_f32[OWN] = made.astype(jnp.float32)

    def take_fixed(phase, which):
        source = ACROSS if which == CORNER else OWN
        fixed_copy(phase, source, ACROSS if which == ACROSS else PEER).wait_recv()
        fixed_f32[which] = fixed[phase, which].astype(jnp.float32)

    def prepare(phase, source, block, first, count, norm, weights, gate):
        span = pl.ds(first, count)
        raw = source[span].astype(jnp.float32)
        normed = layer_norm(flat(raw), norm[...])
        raw_ref[:count, :tokens] = raw
        normed_ref[:count, :tokens] = normed.reshape(count, tokens, channels)
        made = gated(dot(normed.astype(jnp.bfloat16), weights))
        moving[block, span] = made.astype(jnp.float32).reshape(count, tokens, hidden)
        picked = []
        for row in range(count):
            for which in range(QUAD):
                at = pl.ds(mate(which) * rows, SUB)
                picked.append(normed_ref[row, at, :])
                resid[block, first + row, which] = raw_ref[row, at, :]
        picked = jnp.concatenate(picked, axis=0).astype(jnp.bfloat16)
        opened = jax.nn.sigmoid(dot(picked, gate[...]))
        gating[block, span] = opened.reshape(count, QUAD, SUB, channels)

    def multiply(block, first, count, group):
        def one(row, carry):
            right = moving[block, first + row]
            for which in group:
                total = jnp.sum(fixed_f32[which] * right[None], axis=1)
                tri[block, first + row, which, :rows, :] = total
            return carry

        lax.fori_loop(0, count, one, 0)

    def close(phase, jobs, mid, final):
        for job in jobs:
            multiply(*job)

        def gather(ref):
            picked = []
            for block, first, count, group in jobs:
                lanes = slice(group[0], group[-1] + 1)
                picked.append(flat(ref[block, first : first + count, lanes]))
            return jnp.concatenate(picked, axis=0) if len(picked) > 1 else picked[0]

        product = gather(tri).astype(jnp.bfloat16).astype(jnp.float32)
        normed = layer_norm(product, mid[...]).astype(jnp.bfloat16)
        result = gather(resid) + gather(gating) * dot(normed, final[...])
        result = result.astype(jnp.bfloat16)
        at = 0
        for block, first, count, group in jobs:
            size = count * len(group) * SUB
            part = result[at : at + size].reshape(count, len(group), SUB, channels)
            at += size
            span = pl.ds(first, count)
            for place, which in enumerate(group):
                if which == OWN:
                    landed[phase, device(block, OWN), span] = part[:, place]
                else:
                    closed[phase, block, which, span] = part[:, place]
        for block, first, count, group in jobs:
            for which in group:
                if which != OWN:
                    closed_copy(phase, block, which, pl.ds(first, count)).start()

    def exchange(phase, own, norm, weights, gate, mid, final):
        def ready(block, first=0, count=rows):
            source = own if block == SAME else held.at[phase, block]
            prepare(phase, source, block, first, count, norm, weights, gate)

        def join(*jobs):
            close(phase, [(block, 0, rows, group) for block, group in jobs], mid, final)

        def await_line(target, part):
            line_copy(phase, target, part, own).wait_recv()

        def relay(part):
            await_line(OVER, part)
            line_copy(phase, BOTH, part).start()

        ready(SAME)
        take_fixed(phase, PEER)
        join((SAME, NEAR))
        for part in range(pieces):
            await_line(SIDE, part)
        ready(SIDE)
        relay(0)
        relay(1)
        join((SIDE, NEAR))
        relay(2)
        relay(3)
        ready(OVER, 0, 4 * piece)
        relay(4)
        relay(5)
        take_fixed(phase, ACROSS)
        fixed_copy(phase, ACROSS, PEER).start()
        ready(OVER, 4 * piece, 2 * piece)
        join((SAME, (ACROSS,)), (SIDE, (ACROSS,)), (OVER, NEAR + (ACROSS,)))
        take_fixed(phase, CORNER)
        join((SAME, (CORNER,)), (SIDE, (CORNER,)), (OVER, (CORNER,)))
        for part in range(pieces):
            await_line(BOTH, part)
        ready(BOTH)
        join((BOTH, ALL))
        for block in range(blocks):
            for which in (PEER, ACROSS, CORNER):
                closed_wait(phase, block, which)

    def turn(phase, target):
        turned[...] = landed[phase].reshape(tokens * SUB, channels).astype(jnp.float32)
        for row in range(rows):
            target[row] = turned[pl.ds(row, tokens, stride=SUB), :].astype(jnp.bfloat16)

    def finish(phase, own):
        for part in range(pieces):
            for target in (SIDE, OVER, BOTH):
                line_copy(phase, target, part, own).wait_send()
        for block in range(blocks):
            for which in (PEER, ACROSS, CORNER):
                closed_copy(phase, block, which, pl.ds(0, rows)).wait_send()
        fixed_copy(phase, OWN, PEER).wait_send()
        fixed_copy(phase, OWN, ACROSS).wait_send()
        fixed_copy(phase, ACROSS, PEER).wait_send()

    def send_line(phase, own, target):
        for part in range(pieces):
            line_copy(phase, target, part, own).start()

    late = jnp.logical_and(end, core == 0)

    def early_over(phase, own):
        send_line(phase, own, SIDE)

        @pl.when(jnp.logical_not(late))
        def _():
            send_line(phase, own, OVER)

    def launch(phase, own):
        fixed_copy(phase, OWN, ACROSS).start()
        fixed_copy(phase, OWN, PEER).start()

        @pl.when(late)
        def _():
            send_line(phase, own, OVER)

    def load(at):
        return pltpu.make_async_copy(inputs[at], copies[at], loaded.at[at])

    first_inputs = 3
    barrier = pltpu.get_barrier_semaphore()

    def greet(device):
        pl.semaphore_signal(barrier, inc=1, device_id={"axial": device}, device_id_type=MESH)

    for which in (PEER, ACROSS, CORNER):
        greet(mate(which))
    greet(device(SIDE, OWN))
    greet(device(OVER, OWN))
    for at in range(INPUTS):
        load(at).start()
    tri[...] = jnp.zeros_like(tri)
    normed_ref[...] = jnp.zeros_like(normed_ref)
    raw_ref[...] = jnp.zeros_like(raw_ref)
    split = 2 * hidden
    for at in range(first_inputs):
        load(at).wait()
    own_side(0, pair_ref[...], norm_out, proj_out[:, split:])
    pl.semaphore_wait(barrier, QUAD + 1)
    early_over(0, pair_ref)
    launch(0, pair_ref)
    for at in range(first_inputs, INPUTS):
        load(at).wait()
    exchange(0, pair_ref, norm_out, proj_out[:, :split], gate_out, mid_out, final_out)
    middle = held.at[1, SAME]
    turn(0, middle)
    early_over(1, middle)
    own_side(1, middle[...], norm_in, proj_in[:, :split])
    launch(1, middle)
    exchange(1, middle, norm_in, proj_in[:, split:], gate_in, mid_in, final_in)
    turn(1, out_ref)
    finish(0, pair_ref)
    finish(1, middle)


def gather_rows(devices, pair_rep, *weights):
    rows, tokens, channels = pair_rep.shape
    hidden = weights[1].shape[1] // 4
    gains = [w.reshape(1, -1) if w.ndim == 1 else w for w in weights]
    blocks = devices // QUAD
    pieces = PIECES
    block = (rows, tokens, hidden)
    low, full = jnp.bfloat16, jnp.float32
    return pl.pallas_call(
        functools.partial(line_kernel, devices, pieces),
        out_shape=jax.ShapeDtypeStruct(pair_rep.shape, pair_rep.dtype),
        in_specs=[pl.BlockSpec(memory_space=pl.ANY)] * INPUTS,
        out_specs=pl.BlockSpec(memory_space=pltpu.VMEM),
        scratch_shapes=[pltpu.VMEM(array.shape, array.dtype) for array in (pair_rep, *gains)]
        + [
            pltpu.SemaphoreType.DMA((INPUTS,)),
            pltpu.VMEM((2, blocks) + block, low),
            pltpu.VMEM((2, QUAD) + block, low),
            pltpu.VMEM((QUAD,) + block, full),
            pltpu.VMEM((blocks,) + block, full),
            pltpu.VMEM((rows, tokens + SUB, channels), full),
            pltpu.VMEM((rows, tokens + SUB, channels), full),
            pltpu.VMEM((blocks, rows, QUAD, SUB, channels), full),
            pltpu.VMEM((blocks, rows, QUAD, SUB, channels), full),
            pltpu.VMEM((blocks, rows, QUAD, SUB, channels), full),
            pltpu.VMEM((2, blocks, QUAD, rows, SUB, channels), low),
            pltpu.VMEM((2, devices, rows, SUB, channels), low),
            pltpu.VMEM((tokens * SUB, channels), full),
            pltpu.SemaphoreType.DMA((2, blocks, pieces)),
            pltpu.SemaphoreType.DMA((2, blocks, pieces)),
            pltpu.SemaphoreType.DMA((2, QUAD)),
            pltpu.SemaphoreType.DMA((2, QUAD)),
            pltpu.SemaphoreType.DMA((2, blocks, QUAD)),
            pltpu.SemaphoreType.DMA((2, devices)),
        ],
        compiler_params=pltpu.CompilerParams(
            collective_id=0, has_side_effects=True, vmem_limit_bytes=VMEM_BYTES
        ),
        name="gather_rows",
    )(pair_rep, *gains)


def exchange_channels(
    pair_rep,
    norm_out,
    proj_out,
    gate_out,
    mid_out,
    final_out,
    norm_in,
    proj_in,
    gate_in,
    mid_in,
    final_in,
):
    first = update(pair_rep, norm_out, proj_out, gate_out, mid_out, final_out, True)
    return update(first, norm_in, proj_in, gate_in, mid_in, final_in, False)


def solution(mesh):
    devices = mesh.shape["axial"]

    def on_device(*arrays):
        if fits(devices, arrays[0].shape, arrays[2].shape):
            return gather_rows(devices, *arrays)
        return exchange_channels(*arrays)

    placed = (P(("groups", "axial"), None, None), P(), P(), P(), P(), P(), P(), P(), P(), P(), P())
    return jax.shard_map(
        on_device,
        mesh=mesh,
        in_specs=placed,
        out_specs=P(("groups", "axial"), None, None),
        check_vma=False,
    )
```

time: 41.8 us -> 39.6 us (0.947)
  Pallas kernels: 40 us -> 37.9 us
    pallas_call x1, Pallas kernels: 40 us -> 37.9 us  [gather_rows(): pl.pallas_call(functools.partial(line_kernel, devices, pieces), out_shape...]
where the time goes in v2:
time: 39.6 us; the launch traced here: 39.5 us
  Pallas kernels  37.9 us (96%)
  local copies, waits for them, and re-layouts  1.58 us (4%)
    pallas_call x1, Pallas kernels, gather_rows(): pl.pallas_call(functools.partial(line_kernel, devices, pieces), out_shape...  37.9 us
    unnamed x1, local copies, waits for them, and re-layouts  1.58 us

profile of v2, /device:TPU:0, one launch (start us, length us, event | category | flops | bytes accessed | tf_op | source)
XLA Modules:
  0.0 39.5 jit_solution(12409698348100222929)
XLA Ops:
  0.0 37.9 %gather_rows.1 = bf16[6,96,128]{2,1,0:T(8,128)(2,1)} custom-call(bf16[6,96,128]{2,1,0:T(8,128)(2,1)} %refs_0_.1, f32[1,128]{1,0:T(1,128)} %bitcast.4, bf16[128,512]{1,0:T(8,128)(2,1)} %refs_2_.1, bf16[128,128]{1,0:T(8,128)(2,1)} %refs_3_.1, f32[1,128]{1,0:T(1,128)} %bitcast.5, bf16[128,128]{1,0:T(8,128)(2,1)} %refs_5_.1, f32[1,128]{1,0:T(1,128)} %bitcast.6, ...), custom_call_target="tpu_custom_call" | custom-call | tf_op jit(solution)/shard_map/gather_rows/pallas_call | solution.py:414
  37.9 1.6 %copy.13 = bf16[6,96,128]{2,1,0:T(8,128)(2,1)} copy(bf16[6,96,128]{2,1,0:T(8,128)(2,1)} %gather_rows.1) | data formatting | bytes 294912

commit v3 on v2

--- a/solution.py
+++ b/solution.py
@@ -56,8 +56,10 @@
 NEAR, FAR, ALL = (OWN, PEER), (ACROSS, CORNER), (OWN, PEER, ACROSS, CORNER)
 SUB = 8
 HALVES = 2
+PAIR = 2
 INPUTS = 11
 PIECES = 6
+STRIP_PIECES = 3
 VMEM_BYTES = 56 * 1024 * 1024
 
 
@@ -70,6 +72,10 @@
         and devices * rows == tokens
         and rows <= SUB
         and rows % PIECES == 0
+        and rows % PAIR == 0
+        and rows % STRIP_PIECES == 0
+        and tokens % (16 * HALVES) == 0
+        and rows > SUB // 2
         and tokens % 16 == 0
         and channels == hidden
         and hidden % 128 == 0
@@ -112,6 +118,8 @@
     loaded,
     held,
     fixed,
+    strips,
+    fixed_strips,
     fixed_f32,
     moving,
     normed_ref,
@@ -128,6 +136,10 @@
     fixed_recv,
     closed_send,
     closed_recv,
+    strip_send,
+    strip_recv,
+    fixed_strip_send,
+    fixed_strip_recv,
     ) = scratch
     rows, tokens, channels = pair_ref.shape
     hidden = fixed.shape[-1]
@@ -191,8 +203,8 @@
     def closed_copy(phase, block, which, span):
         here = device(block, OWN)
         return remote(
-            closed.at[phase, block, which, span],
-            landed.at[phase, here, span],
+            closed.at[phase, block, which, span, pl.ds(0, rows)],
+            landed.at[phase, here, span, pl.ds(0, rows)],
             closed_send.at[phase, block, which],
             closed_recv.at[phase, here],
             mate(which),
@@ -201,12 +213,79 @@
     def closed_wait(phase, block, which):
         there = device(block, which)
         remote(
-            closed.at[phase, block, which],
-            landed.at[phase, there],
+            closed.at[phase, block, which, :, pl.ds(0, rows)],
+            landed.at[phase, there, :, pl.ds(0, rows)],
             closed_send.at[phase, block, which],
             closed_recv.at[phase, there],
             mate(which),
         ).wait_recv()
+
+    width = tokens // HALVES
+    thick = rows // STRIP_PIECES
+
+    def strip_copy(target, chunk, part):
+        span = pl.ds(part * thick, thick)
+        lands = 1 - chunk if target == OVER else chunk
+        return remote(
+            strips.at[OVER if target == BOTH else SAME, chunk, span],
+            strips.at[target, lands, span],
+            strip_send.at[target, chunk, part],
+            strip_recv.at[target, lands, part],
+            device(OVER if target == OVER else SIDE, OWN),
+        )
+
+    def strip_wait(target, chunk, part):
+        strip_copy(target, 1 - chunk if target == OVER else chunk, part).wait_recv()
+
+    def fixed_strip_copy(which, to, chunk):
+        arrives = {(OWN, PEER): PEER, (OWN, ACROSS): ACROSS, (ACROSS, PEER): CORNER}[which, to]
+        return remote(
+            fixed_strips.at[which, chunk],
+            fixed_strips.at[arrives, chunk],
+            fixed_strip_send.at[arrives, chunk],
+            fixed_strip_recv.at[arrives, chunk],
+            mate(to),
+        )
+
+    def columns(chunk):
+        return slice(chunk * width, (chunk + 1) * width)
+
+    def send_strip(chunk):
+        for part in range(STRIP_PIECES):
+            strip_copy(OVER, chunk, part).start()
+            strip_copy(SIDE, chunk, part).start()
+
+    def relay_strip(chunk, part):
+        strip_wait(OVER, chunk, part)
+        strip_copy(BOTH, chunk, part).start()
+
+    def await_strip(target, chunk):
+        for part in range(STRIP_PIECES):
+            strip_wait(target, chunk, part)
+
+    def take_fixed_strip(which, chunk):
+        source = ACROSS if which == CORNER else OWN
+        fixed_strip_copy(source, ACROSS if which == ACROSS else PEER, chunk).wait_recv()
+        fixed_f32[which, :, columns(chunk), :] = fixed_strips[which, chunk].astype(jnp.float32)
+
+    def own_strip(chunk, norm, weights):
+        values = flat(strips[SAME, chunk]).astype(jnp.float32)
+        normed = layer_norm(values, norm[...]).astype(jnp.bfloat16)
+        made = gated(dot(normed, weights)).reshape(rows, width, hidden)
+        fixed_strips[OWN, chunk] = made
+        fixed_f32[OWN, :, columns(chunk), :] = made.astype(jnp.float32)
+        fixed_strip_copy(OWN, ACROSS, chunk).start()
+        fixed_strip_copy(OWN, PEER, chunk).start()
+
+    def turn_strip(chunk):
+        group = devices // HALVES
+        base = (half if chunk == 0 else 1 - half) * group
+        size = group * rows * SUB
+        picked = landed[0, pl.ds(base, group)].reshape(size, channels)
+        turned[:size] = picked.astype(jnp.float32)
+        for row in range(rows):
+            taken = turned[pl.ds(row, width, stride=SUB), :]
+            strips[SAME, chunk, row] = taken.astype(jnp.bfloat16)
 
     def flat(values):
         return values.reshape(-1, values.shape[-1])
@@ -243,19 +322,64 @@
         opened = jax.nn.sigmoid(dot(picked, gate[...]))
         gating[block, span] = opened.reshape(count, QUAD, SUB, channels)
 
-    def multiply(block, first, count, group):
-        def one(row, carry):
-            right = moving[block, first + row]
-            for which in group:
-                total = jnp.sum(fixed_f32[which] * right[None], axis=1)
-                tri[block, first + row, which, :rows, :] = total
+    def prepare_strip(block, chunk, norm, weights, gate):
+        raw = strips[block, chunk].astype(jnp.float32)
+        normed = layer_norm(flat(raw), norm[...])
+        made = gated(dot(normed.astype(jnp.bfloat16), weights))
+        made = made.astype(jnp.float32).reshape(rows, width, hidden)
+        moving[block, :, columns(chunk), :] = made
+        if chunk:
+            return
+        raw_ref[:, :width] = raw
+        normed_ref[:, :width] = normed.reshape(rows, width, channels)
+        picked = []
+        for row in range(rows):
+            for which in range(QUAD):
+                at = pl.ds((mate(which) - half * (devices // HALVES)) * rows, SUB)
+                picked.append(normed_ref[row, at, :])
+                resid[block, row, which] = raw_ref[row, at, :]
+        picked = jnp.concatenate(picked, axis=0).astype(jnp.bfloat16)
+        opened = jax.nn.sigmoid(dot(picked, gate[...]))
+        gating[block] = opened.reshape(rows, QUAD, SUB, channels)
+
+    def fold(parts):
+        place = lax.broadcasted_iota(jnp.int32, (SUB, hidden), 0)
+        apart = SUB // 2
+        while apart:
+            first_half = (place // apart) % 2 == 0
+
+            def joined(low, high):
+                ahead = low + pltpu.roll(low, SUB - apart, 0)
+                if high is None:
+                    return jnp.where(first_half, ahead, low + pltpu.roll(low, apart, 0))
+                return jnp.where(first_half, ahead, high + pltpu.roll(high, apart, 0))
+
+            parts = parts + [None] * (2 * apart - len(parts))
+            parts = [joined(parts[at], parts[at + apart]) for at in range(apart)]
+            apart //= 2
+        return parts[0]
+
+    def tiles(values):
+        return values.reshape(tokens // SUB, SUB, hidden)
+
+    def multiply(jobs):
+        def one(at, carry):
+            for block, group in jobs:
+                right = [tiles(moving[block, PAIR * at + row]) for row in range(PAIR)]
+                for which in group:
+                    sums = [[], []]
+                    for own in range(rows):
+                        left = tiles(fixed_f32[which, own])
+                        for row in range(PAIR):
+                            sums[row].append(jnp.sum(left * right[row], axis=0))
+                    for row in range(PAIR):
+                        tri[block, PAIR * at + row, which] = fold(sums[row])
             return carry
 
-        lax.fori_loop(0, count, one, 0)
+        lax.fori_loop(0, rows // PAIR, one, 0)
 
     def close(phase, jobs, mid, final):
-        for job in jobs:
-            multiply(*job)
+        multiply([(block, group) for block, _, _, group in jobs])
 
         def gather(ref):
             picked = []
@@ -299,33 +423,115 @@
             await_line(OVER, part)
             line_copy(phase, BOTH, part).start()
 
+        def await_all(target):
+            for part in range(pieces):
+                await_line(target, part)
+
+        def take_across():
+            take_fixed(phase, ACROSS)
+            fixed_copy(phase, ACROSS, PEER).start()
+
+        def hand_on():
+            landed_wait(phase, (SAME, SIDE))
+            turn_strip(0)
+            send_strip(0)
+
         ready(SAME)
         take_fixed(phase, PEER)
         join((SAME, NEAR))
-        for part in range(pieces):
-            await_line(SIDE, part)
-        ready(SIDE)
-        relay(0)
-        relay(1)
-        join((SIDE, NEAR))
-        relay(2)
-        relay(3)
-        ready(OVER, 0, 4 * piece)
-        relay(4)
-        relay(5)
-        take_fixed(phase, ACROSS)
-        fixed_copy(phase, ACROSS, PEER).start()
-        ready(OVER, 4 * piece, 2 * piece)
-        join((SAME, (ACROSS,)), (SIDE, (ACROSS,)), (OVER, NEAR + (ACROSS,)))
-        take_fixed(phase, CORNER)
-        join((SAME, (CORNER,)), (SIDE, (CORNER,)), (OVER, (CORNER,)))
-        for part in range(pieces):
-            await_line(BOTH, part)
-        ready(BOTH)
-        join((BOTH, ALL))
-        for block in range(blocks):
+
+        @pl.when(end)
+        def _():
+            take_across()
+            await_all(SIDE)
+            ready(SIDE)
+            join((SAME, (ACROSS,)), (SIDE, NEAR + (ACROSS,)))
+            relay(0)
+            relay(1)
+            take_fixed(phase, CORNER)
+            join((SAME, (CORNER,)), (SIDE, (CORNER,)))
+            relay(2)
+            relay(3)
+            ready(OVER, 0, 4 * piece)
+            relay(4)
+            relay(5)
+            ready(OVER, 4 * piece, 2 * piece)
+            join((OVER, ALL))
+            await_all(BOTH)
+            ready(BOTH)
+            join((BOTH, FAR))
+            hand_on()
+            join((BOTH, NEAR))
+
+        @pl.when(jnp.logical_not(end))
+        def _():
+            fixed_copy(phase, OWN, ACROSS).wait_send()
+            send_line(phase, own, OVER)
+            for part in range(pieces):
+                relay(part)
+            ready(OVER)
+            join((OVER, NEAR))
+            await_all(SIDE)
+            ready(SIDE)
+            join((SIDE, NEAR))
+            take_across()
+            join((SAME, (ACROSS,)), (SIDE, (ACROSS,)))
+            await_all(BOTH)
+            ready(BOTH)
+            take_fixed(phase, CORNER)
+            join((SAME, (CORNER,)), (SIDE, (CORNER,)))
+            join((OVER, FAR), (BOTH, FAR))
+            hand_on()
+            join((BOTH, NEAR))
+
+    def landed_wait(phase, picked):
+        for block in picked:
             for which in (PEER, ACROSS, CORNER):
                 closed_wait(phase, block, which)
+
+    def exchange_strips(norm, own_weights, weights, gate, mid, final):
+        def ready(block, chunk):
+            prepare_strip(block, chunk, norm, weights, gate)
+
+        def join(*jobs):
+            close(1, [(block, 0, rows, group) for block, group in jobs], mid, final)
+
+        own_strip(0, norm, own_weights)
+        ready(SAME, 0)
+        landed_wait(0, (OVER, BOTH))
+        turn_strip(1)
+        send_strip(1)
+        own_strip(1, norm, own_weights)
+        ready(SAME, 1)
+        for chunk in range(HALVES):
+            take_fixed_strip(PEER, chunk)
+        join((SAME, NEAR))
+        for part in range(STRIP_PIECES):
+            relay_strip(1, part)
+        await_strip(SIDE, 0)
+        ready(SIDE, 0)
+        ready(OVER, 1)
+        await_strip(SIDE, 1)
+        ready(SIDE, 1)
+        join((SIDE, NEAR))
+        relay_strip(0, 0)
+        for chunk in range(HALVES):
+            take_fixed_strip(ACROSS, chunk)
+            fixed_strip_copy(ACROSS, PEER, chunk).start()
+        relay_strip(0, 1)
+        join((SAME, (ACROSS,)), (SIDE, (ACROSS,)))
+        relay_strip(0, 2)
+        ready(OVER, 0)
+        await_strip(BOTH, 1)
+        ready(BOTH, 1)
+        for chunk in range(HALVES):
+            take_fixed_strip(CORNER, chunk)
+        join((SAME, (CORNER,)), (SIDE, (CORNER,)), (OVER, ALL))
+        await_strip(BOTH, 0)
+        ready(BOTH, 0)
+        join((BOTH, FAR))
+        join((BOTH, NEAR))
+        landed_wait(1, (SAME, SIDE, OVER, BOTH))
 
     def turn(phase, target):
         turned[...] = landed[phase].reshape(tokens * SUB, channels).astype(jnp.float32)
@@ -336,33 +542,34 @@
         for part in range(pieces):
             for target in (SIDE, OVER, BOTH):
                 line_copy(phase, target, part, own).wait_send()
+        fixed_copy(phase, OWN, PEER).wait_send()
+
+        @pl.when(end)
+        def _():
+            fixed_copy(phase, OWN, ACROSS).wait_send()
+
+        fixed_copy(phase, ACROSS, PEER).wait_send()
+        finish_closed(phase)
+
+    def finish_closed(phase):
         for block in range(blocks):
             for which in (PEER, ACROSS, CORNER):
                 closed_copy(phase, block, which, pl.ds(0, rows)).wait_send()
-        fixed_copy(phase, OWN, PEER).wait_send()
-        fixed_copy(phase, OWN, ACROSS).wait_send()
-        fixed_copy(phase, ACROSS, PEER).wait_send()
 
     def send_line(phase, own, target):
         for part in range(pieces):
             line_copy(phase, target, part, own).start()
 
-    late = jnp.logical_and(end, core == 0)
-
     def early_over(phase, own):
         send_line(phase, own, SIDE)
 
-        @pl.when(jnp.logical_not(late))
+        @pl.when(end)
         def _():
             send_line(phase, own, OVER)
 
     def launch(phase, own):
         fixed_copy(phase, OWN, ACROSS).start()
         fixed_copy(phase, OWN, PEER).start()
-
-        @pl.when(late)
-        def _():
-            send_line(phase, own, OVER)
 
     def load(at):
         return pltpu.make_async_copy(inputs[at], copies[at], loaded.at[at])
@@ -392,15 +599,17 @@
     for at in range(first_inputs, INPUTS):
         load(at).wait()
     exchange(0, pair_ref, norm_out, proj_out[:, :split], gate_out, mid_out, final_out)
-    middle = held.at[1, SAME]
-    turn(0, middle)
-    early_over(1, middle)
-    own_side(1, middle[...], norm_in, proj_in[:, :split])
-    launch(1, middle)
-    exchange(1, middle, norm_in, proj_in[:, split:], gate_in, mid_in, final_in)
+    exchange_strips(norm_in, proj_in[:, :split], proj_in[:, split:], gate_in, mid_in, final_in)
     turn(1, out_ref)
     finish(0, pair_ref)
-    finish(1, middle)
+    for chunk in range(HALVES):
+        for part in range(STRIP_PIECES):
+            for target in (SIDE, OVER, BOTH):
+                strip_copy(target, chunk, part).wait_send()
+        fixed_strip_copy(OWN, PEER, chunk).wait_send()
+        fixed_strip_copy(OWN, ACROSS, chunk).wait_send()
+        fixed_strip_copy(ACROSS, PEER, chunk).wait_send()
+    finish_closed(1)
 
 
 def gather_rows(devices, pair_rep, *weights):
@@ -419,8 +628,10 @@
         scratch_shapes=[pltpu.VMEM(array.shape, array.dtype) for array in (pair_rep, *gains)]
         + [
             pltpu.SemaphoreType.DMA((INPUTS,)),
-            pltpu.VMEM((2, blocks) + block, low),
-            pltpu.VMEM((2, QUAD) + block, low),
+            pltpu.VMEM((1, blocks) + block, low),
+            pltpu.VMEM((1, QUAD) + block, low),
+            pltpu.VMEM((blocks, HALVES, rows, tokens // HALVES, channels), low),
+            pltpu.VMEM((QUAD, HALVES, rows, tokens // HALVES, hidden), low),
             pltpu.VMEM((QUAD,) + block, full),
             pltpu.VMEM((blocks,) + block, full),
             pltpu.VMEM((rows, tokens + SUB, channels), full),
@@ -437,6 +648,10 @@
             pltpu.SemaphoreType.DMA((2, QUAD)),
             pltpu.SemaphoreType.DMA((2, blocks, QUAD)),
             pltpu.SemaphoreType.DMA((2, devices)),
+            pltpu.SemaphoreType.DMA((blocks, HALVES, STRIP_PIECES)),
+            pltpu.SemaphoreType.DMA((blocks, HALVES, STRIP_PIECES)),
+            pltpu.SemaphoreType.DMA((QUAD, HALVES)),
+            pltpu.SemaphoreType.DMA((QUAD, HALVES)),
         ],
         compiler_params=pltpu.CompilerParams(
             collective_id=0, has_side_effects=True, vmem_limit_bytes=VMEM_BYTES

time: 39.6 us -> 37.4 us (0.944)
  Pallas kernels: 37.9 us -> 35.7 us
    pallas_call x1, Pallas kernels: 37.9 us -> 35.7 us  [gather_rows(): pl.pallas_call(functools.partial(line_kernel, devices, pieces), out_shape...]
where the time goes in v3:
time: 37.4 us; the launch traced here: 37.3 us
  Pallas kernels  35.7 us (95%)
  local copies, waits for them, and re-layouts  1.58 us (4%)
    pallas_call x1, Pallas kernels, gather_rows(): pl.pallas_call(functools.partial(line_kernel, devices, pieces), out_shape...  35.7 us
    unnamed x1, local copies, waits for them, and re-layouts  1.58 us

profile of v3, /device:TPU:0, one launch (start us, length us, event | category | flops | bytes accessed | tf_op | source)
XLA Modules:
  0.0 37.3 jit_solution(4743056294935643081)
XLA Ops:
  0.0 35.7 %gather_rows.1 = bf16[6,96,128]{2,1,0:T(8,128)(2,1)} custom-call(bf16[6,96,128]{2,1,0:T(8,128)(2,1)} %refs_0_.1, f32[1,128]{1,0:T(1,128)} %bitcast.4, bf16[128,512]{1,0:T(8,128)(2,1)} %refs_2_.1, bf16[128,128]{1,0:T(8,128)(2,1)} %refs_3_.1, f32[1,128]{1,0:T(1,128)} %bitcast.5, bf16[128,128]{1,0:T(8,128)(2,1)} %refs_5_.1, f32[1,128]{1,0:T(1,128)} %bitcast.6, ...), custom_call_target="tpu_custom_call" | custom-call | tf_op jit(solution)/shard_map/gather_rows/pallas_call | solution.py:623
  35.7 1.6 %copy.13 = bf16[6,96,128]{2,1,0:T(8,128)(2,1)} copy(bf16[6,96,128]{2,1,0:T(8,128)(2,1)} %gather_rows.1) | data formatting | bytes 294912

commit v4 on v3

--- a/solution.py
+++ b/solution.py
@@ -452,10 +452,9 @@
             join((SAME, (CORNER,)), (SIDE, (CORNER,)))
             relay(2)
             relay(3)
-            ready(OVER, 0, 4 * piece)
             relay(4)
             relay(5)
-            ready(OVER, 4 * piece, 2 * piece)
+            ready(OVER)
             join((OVER, ALL))
             await_all(BOTH)
             ready(BOTH)

time: 37.4 us -> 37.3 us (level)
  no operation moved by 1% of the time
where the time goes in v4:
time: 37.3 us; the launch traced here: 37.2 us
  Pallas kernels  35.6 us (95%)
  local copies, waits for them, and re-layouts  1.58 us (4%)
    pallas_call x1, Pallas kernels, gather_rows(): pl.pallas_call(functools.partial(line_kernel, devices, pieces), out_shape...  35.6 us
    unnamed x1, local copies, waits for them, and re-layouts  1.58 us

profile of v4, /device:TPU:0, one launch (start us, length us, event | category | flops | bytes accessed | tf_op | source)
XLA Modules:
  0.0 37.2 jit_solution(18084706124086658925)
XLA Ops:
  0.0 35.6 %gather_rows.1 = bf16[6,96,128]{2,1,0:T(8,128)(2,1)} custom-call(bf16[6,96,128]{2,1,0:T(8,128)(2,1)} %refs_0_.1, f32[1,128]{1,0:T(1,128)} %bitcast.4, bf16[128,512]{1,0:T(8,128)(2,1)} %refs_2_.1, bf16[128,128]{1,0:T(8,128)(2,1)} %refs_3_.1, f32[1,128]{1,0:T(1,128)} %bitcast.5, bf16[128,128]{1,0:T(8,128)(2,1)} %refs_5_.1, f32[1,128]{1,0:T(1,128)} %bitcast.6, ...), custom_call_target="tpu_custom_call" | custom-call | tf_op jit(solution)/shard_map/gather_rows/pallas_call | solution.py:622
  35.6 1.6 %copy.13 = bf16[6,96,128]{2,1,0:T(8,128)(2,1)} copy(bf16[6,96,128]{2,1,0:T(8,128)(2,1)} %gather_rows.1) | data formatting | bytes 294912

commit v5 on v4

--- a/solution.py
+++ b/solution.py
@@ -533,7 +533,7 @@
         landed_wait(1, (SAME, SIDE, OVER, BOTH))
 
     def turn(phase, target):
-        turned[...] = landed[phase].reshape(tokens * SUB, channels).astype(jnp.float32)
+        turned[: tokens * SUB] = landed[phase].reshape(tokens * SUB, channels).astype(jnp.float32)
         for row in range(rows):
             target[row] = turned[pl.ds(row, tokens, stride=SUB), :].astype(jnp.bfloat16)
 
@@ -640,7 +640,7 @@
             pltpu.VMEM((blocks, rows, QUAD, SUB, channels), full),
             pltpu.VMEM((2, blocks, QUAD, rows, SUB, channels), low),
             pltpu.VMEM((2, devices, rows, SUB, channels), low),
-            pltpu.VMEM((tokens * SUB, channels), full),
+            pltpu.VMEM(((tokens + SUB) * SUB, channels), full),
             pltpu.SemaphoreType.DMA((2, blocks, pieces)),
             pltpu.SemaphoreType.DMA((2, blocks, pieces)),
             pltpu.SemaphoreType.DMA((2, QUAD)),

time: 37.3 us -> 37.3 us (level)
  no operation moved by 1% of the time
where the time goes in v5:
time: 37.3 us; the launch traced here: 37.2 us
  Pallas kernels  35.6 us (95%)
  local copies, waits for them, and re-layouts  1.58 us (4%)
    pallas_call x1, Pallas kernels, gather_rows(): pl.pallas_call(functools.partial(line_kernel, devices, pieces), out_shape...  35.6 us
    unnamed x1, local copies, waits for them, and re-layouts  1.58 us

profile of v5, /device:TPU:0, one launch (start us, length us, event | category | flops | bytes accessed | tf_op | source)
XLA Modules:
  0.0 37.2 jit_solution(7497441902506102063)
XLA Ops:
  0.0 35.6 %gather_rows.1 = bf16[6,96,128]{2,1,0:T(8,128)(2,1)} custom-call(bf16[6,96,128]{2,1,0:T(8,128)(2,1)} %refs_0_.1, f32[1,128]{1,0:T(1,128)} %bitcast.4, bf16[128,512]{1,0:T(8,128)(2,1)} %refs_2_.1, bf16[128,128]{1,0:T(8,128)(2,1)} %refs_3_.1, f32[1,128]{1,0:T(1,128)} %bitcast.5, bf16[128,128]{1,0:T(8,128)(2,1)} %refs_5_.1, f32[1,128]{1,0:T(1,128)} %bitcast.6, ...), custom_call_target="tpu_custom_call" | custom-call | tf_op jit(solution)/shard_map/gather_rows/pallas_call | solution.py:622
  35.6 1.6 %copy.13 = bf16[6,96,128]{2,1,0:T(8,128)(2,1)} copy(bf16[6,96,128]{2,1,0:T(8,128)(2,1)} %gather_rows.1) | data formatting | bytes 294912
